TPU v7x, 32 devices: a whole 2x2x4 slice. The times are simulated.
32 devices in a mesh: prow: 4 (over y, core), pcol: 8 (over z, x).
Axes of the slice: x: 2, y: 2, z: 4, core: 2. Of those that a mesh axis runs over, the one named last changes fastest.
Arguments:
- tiles: bfloat16 [4, 8, 16, 256, 256], P('prow', 'pcol'), may hold values from -6 to 6
- tile_ids: int32 [4, 8, 16], P('prow', 'pcol'), may hold values from 0 to 127, as said below
- counts: int32 [4, 8], P('prow', 'pcol'), may hold values from 1 to 16, as said below
- pivots: int32 [256], replicated, may hold values from 0 to 16383, as said below
- l_inverse: bfloat16 [256, 256], P(None, 'pcol'), may hold values from -1 to 1, as said below
- u_inverse: bfloat16 [256, 256], P('prow'), may hold values from -0.125 to 0.5, as said below
Outputs:
- factored: bfloat16 [4, 8, 16, 256, 256], P('prow', 'pcol')
Inputs may be any that keep to these rules, and one draw needn't show every extreme that they name: Live slot s of device (p, q) holds local tile row tile_ids[p, q, s] // 8 and local tile column tile_ids[p, q, s] % 8; live codes of one device are distinct, padded slots hold arbitrary codes. Let R be the tile rows I >= 1 with tile (I, 0) held and C the tile columns J >= 1 with tile (0, J) held. Tile (0, 0) is held; on each prow index R takes the last one to 3 local tile rows, on each pcol index C takes the last one to 3 local tile columns, and both most counts are reached on some index. Every tile whose row is 0 or in R and whose column is 0 or in C is held; no other held tile lies in tile row 0, a tile row of R, or tile column 0. `counts`: some device has 16 live slots. Row r of tile row 0 and row pivots[r] change places; pivots[r] is r or a row of a tile row of R, and the values that differ from their r are distinct. `l_inverse`: lower triangular with unit diagonal. `u_inverse`: upper triangular with a positive diagonal.
All inputs are finite; a program needn't handle non-finite values.
Results may differ from a plain program's by a relative error of at most 0.0056.
Values may be sent and summed in bfloat16 or wider, within the bound.
A program may use at most 64 MiB of HBM per device.

v0:
```python
import jax
import jax.numpy as jnp
from jax import lax
from jax.sharding import PartitionSpec as P

TILE_SIDE = 256
LOCAL_ROWS = 16
TILE_SLOTS = 16
LOWER_MOST = 3
UPPER_MOST = 3


def broadcast(value, axis, source):
    kept = jnp.where(lax.axis_index(axis) == source, value, 0).astype(value.dtype)
    return lax.psum(kept, axis)


def pick_rows(tile, rows):
    return tile[rows]


def body(tiles, tile_ids, counts, pivots, l_inverse, u_inverse):
    row_count = lax.axis_size("prow")
    col_count = lax.axis_size("pcol")
    my_row = lax.axis_index("prow")
    my_col = lax.axis_index("pcol")
    grid_cols = LOCAL_ROWS * row_count // col_count
    total_rows = LOCAL_ROWS * row_count * TILE_SIDE
    local = tiles[0, 0]
    codes = tile_ids[0, 0]
    slot_range = jnp.arange(TILE_SLOTS, dtype=jnp.int32)
    alive = slot_range < counts[0, 0]
    loc_row = codes // grid_cols
    loc_col = codes % grid_cols
    glob_row = my_row + row_count * loc_row
    glob_col = my_col + col_count * loc_col
    col_range = jnp.arange(grid_cols, dtype=jnp.int32)
    upper_inv = lax.all_gather(u_inverse, "prow", axis=0, tiled=True)
    lower_inv = lax.all_gather(l_inverse, "pcol", axis=1, tiled=True)
    source_tile = pivots // TILE_SIDE
    source_row = pivots % TILE_SIDE
    gathered = local[:, source_row, :]
    owned = (source_tile[None, :] == glob_row[:, None]) & alive[:, None]
    contrib = jnp.where(owned[:, :, None], gathered, jnp.zeros_like(gathered))
    col_hot = ((loc_col[:, None] == col_range[None, :]) & alive[:, None]).astype(jnp.bfloat16)
    top_flag = (glob_row == 0).astype(jnp.bfloat16)
    top_hot = col_hot * top_flag[:, None]
    flag_part = jnp.sum(
        top_hot.astype(jnp.float32) * (glob_col >= 1).astype(jnp.float32)[:, None], axis=0
    )
    new_part = jnp.einsum("sj,srb->jrb", col_hot, contrib, preferred_element_type=jnp.float32)
    old_part = jnp.einsum("sj,srb->jrb", top_hot, local, preferred_element_type=jnp.float32)
    new_sum, old_sum, flag_sum = (
        lax.psum(new_part.astype(jnp.bfloat16), "prow").astype(jnp.float32),
        lax.psum(old_part.astype(jnp.bfloat16), "prow").astype(jnp.float32),
        lax.psum(flag_part.astype(jnp.bfloat16), "prow").astype(jnp.float32),
    )
    new_top = new_sum.astype(jnp.bfloat16)
    old_top = old_sum.astype(jnp.bfloat16)
    anchor_top = (
        jnp.full((total_rows,), -1, jnp.int32)
        .at[pivots]
        .set(jnp.arange(TILE_SIDE, dtype=jnp.int32))
    )
    row_index = glob_row[:, None] * TILE_SIDE + jnp.arange(TILE_SIDE, dtype=jnp.int32)[None, :]
    anchor = anchor_top[row_index]
    moved = (anchor >= 0) & (glob_row >= 1)[:, None]
    from_top = jax.vmap(pick_rows)(old_top[loc_col], jnp.maximum(anchor, 0))
    swapped = jnp.where(moved[:, :, None], from_top, local)
    primed = jnp.where((glob_row == 0)[:, None, None], new_top[loc_col], swapped)
    panel_mask = alive & (glob_col == 0) & (glob_row >= 1)
    panel_slots = jnp.argsort(jnp.where(panel_mask, 0, 1), stable=True)[:LOWER_MOST]
    panel_valid = panel_mask[panel_slots]
    lower_full = jnp.einsum(
        "kab,bc->kac", primed[panel_slots], upper_inv, preferred_element_type=jnp.float32
    )
    lower_list = jnp.where(panel_valid[:, None, None], lower_full, 0.0).astype(jnp.bfloat16)
    lower_rows = jnp.where(panel_valid, loc_row[panel_slots], -1)
    got_list, got_rows = (broadcast(lower_list, "pcol", 0), broadcast(lower_rows, "pcol", 0))
    row_match = got_rows[None, :] == loc_row[:, None]
    lower_pick = jnp.sum(
        jnp.where(row_match, jnp.arange(LOWER_MOST, dtype=jnp.int32)[None, :], 0), axis=1
    )
    lower_present = jnp.any(row_match, axis=1)
    column_flags = flag_sum > 0.5
    column_order = jnp.argsort(jnp.where(column_flags, 0, 1), stable=True)[:UPPER_MOST]
    upper_valid = column_flags[column_order]
    upper_full = jnp.einsum(
        "ab,kbc->kac", lower_inv, new_top[column_order], preferred_element_type=jnp.float32
    )
    upper_list = jnp.where(upper_valid[:, None, None], upper_full, 0.0).astype(jnp.bfloat16)
    upper_ids = jnp.where(upper_valid, column_order, -1)
    col_match = upper_ids[None, :] == loc_col[:, None]
    upper_pick = jnp.sum(
        jnp.where(col_match, jnp.arange(UPPER_MOST, dtype=jnp.int32)[None, :], 0), axis=1
    )
    upper_present = jnp.any(col_match, axis=1)
    result = jnp.where(alive[:, None, None], primed, jnp.zeros_like(primed))
    upper_mask = alive & (glob_row == 0) & (glob_col >= 1)
    result = jnp.where(upper_mask[:, None, None], upper_list[upper_pick], result)
    result = result.at[panel_slots].set(
        jnp.where(panel_valid[:, None, None], lower_list, result[panel_slots])
    )
    needs = alive & (glob_row >= 1) & (glob_col >= 1) & lower_present & upper_present
    order = jnp.argsort(jnp.where(needs, 0, 1), stable=True)
    needed = jnp.sum(needs.astype(jnp.int32))

    def trailing(current, lower_tile, upper_index):
        product = jnp.dot(lower_tile, upper_list[upper_index], preferred_element_type=jnp.float32)
        return (current.astype(jnp.float32) - product).astype(jnp.bfloat16)

    def own_step(position, held):
        slot = order[position]
        value = trailing(primed[slot], got_list[lower_pick[slot]], upper_pick[slot])
        return held.at[slot].set(value)

    result = lax.fori_loop(0, needed, own_step, result)
    return result[None, None]


def solution(mesh):
    placed = (
        P("prow", "pcol", None, None, None),
        P("prow", "pcol", None),
        P("prow", "pcol"),
        P(),
        P(None, "pcol"),
        P("prow", None),
    )
    return jax.shard_map(
        body,
        mesh=mesh,
        in_specs=placed,
        out_specs=P("prow", "pcol", None, None, None),
        check_vma=False,
    )
```

profile of v0, /device:TPU:0, one launch (start us, length us, event | category | flops | bytes accessed | tf_op | source)
XLA Modules:
  0.0 367.1 jit_solution(17851985653120215926)
XLA Ops:
  7.2 2.9 copy.87
  10.2 2.2 convolution_convert_fusion
  12.8 2.1 gather_fusion.1
  14.9 3.0 fusion.11
  17.9 8.4 %psum.35 = bf16[8]{0:T(256)(128)(2,1)S(1)} all-reduce(bf16[8]{0:T(256)(128)(2,1)S(1)} %multiply_reduce_fusion), channel_id=1, replica_groups=mesh['prow'=4,'pcol'=8] {'prow'}, use_global_device_ids=true, to_apply=%region_1.2 | all-reduce | flops 8 | bytes 32 | tf_op jit(solution)/shard_map/psum | solution.py:56
  26.4 1.0 sort.48
  28.0 1.2 sort.49
  30.6 11.6 %psum.38 = s32[3]{0:T(128)S(1)} all-reduce(s32[3]{0:T(128)S(1)} %broadcast_select_fusion.2), channel_id=1, replica_groups=mesh['prow'=4,'pcol'=8] {'pcol'}, use_global_device_ids=true, to_apply=%region_9.10 | all-reduce | flops 3 | bytes 24 | tf_op jit(solution)/shard_map/psum | solution.py:15
  42.5 1.4 scatter_custom_fusion
  43.9 23.0 %gather_fusion.5 = s32[4096]{0:T(1024)S(1)} fusion(s32[16384]{0:T(1024)S(1)} %scatter_custom_fusion, s32[4096]{0:T(1024)S(1)} %broadcast_clamp_fusion), kind=kCustom, calls=%fused_computation.5 | custom fusion | bytes 49152 | tf_op jit(solution)/shard_map/gather | solution.py:66
  67.3 6.0 %all_gather.7 = bf16[256,256]{1,0:T(8,128)(2,1)S(1)} all-gather(bf16[64,256]{1,0:T(8,128)(2,1)S(1)} %copy-done.4), channel_id=1, replica_groups=mesh['prow'=4,'pcol'=8] {'prow'}, dimensions={0}, use_global_device_ids=true | all-gather | bytes 163840 | tf_op jit(solution)/shard_map/all_gather | solution.py:38
  73.2 30.7 %all_gather.6 = bf16[256,256]{0,1:T(8,128)(2,1)S(1)} all-gather(bf16[256,32]{0,1:T(8,128)(2,1)S(1)} %copy-done.5), channel_id=1, replica_groups=mesh['prow'=4,'pcol'=8] {'pcol'}, dimensions={1}, use_global_device_ids=true | all-gather | bytes 147456 | tf_op jit(solution)/shard_map/all_gather | solution.py:39
  104.1 1.5 copy.63
  105.9 1.3 gather_fusion.2
  107.2 2.0 gather_fusion.4
  109.2 0.7 gather_fusion.6
  109.9 1.3 fusion.14
  111.4 40.7 %gather_fusion.11 = bf16[4096,256]{1,0:T(8,128)(2,1)} fusion(bf16[16,256,256]{2,1,0:T(8,128)(2,1)S(1)} %gather_fusion.6, s32[4096]{0:T(1024)S(1)} %bitcast.105), kind=kCustom, calls=%fused_computation.11 | custom fusion | bytes 4227072 | tf_op jit(solution)/shard_map/vmap()/gather | solution.py:19
  152.1 2.0 gather_fusion.3
  154.1 16.0 %copy_select_fusion = (bf16[16,256,256]{2,0,1:T(8,128)(2,1)}, bf16[16,256,256]{2,0,1:T(8,128)(2,1)S(1)}) fusion(bf16[16,256,256]{2,1,0:T(8,128)(2,1)} %gather_fusion.3, pred[16]{0:T(512)(128)(4,1)S(1)} %iota_compare_fusion.1, pred[16]{0:T(512)(128)(4,1)S(1)} %get-tuple-element.155, bf16[1,1,16,256,256]{4,3,2,1,0:T(8,128)(2,1)S(1)} %copy-done.1, ...), kind=kLoop, calls=%fused_computation.27 | loop fusion | flops 4194304 | bytes 12587056 | tf_op jit(solution)/shard_map/jit(_where)/select_n | solution.py:100
  170.1 2.1 copy.67
  172.2 2.2 gather_fusion.8
  174.4 2.1 copy.69
  176.5 2.2 gather_fusion.9
  178.7 1.0 broadcast_select_fusion.1
  179.7 1.3 sort.50
  181.0 0.7 convert_reduce_fusion
  181.8 2.4 scatter_fusion
  184.2 64.8 %all-reduce.4.cloned.1.call-done = bf16[3,256,256]{2,1,0:T(8,128)(2,1)} async-done(((bf16[3,256,256]{2,1,0:T(8,128)(2,1)}), bf16[3,256,256]{2,1,0:T(8,128)(2,1)}) %all-reduce.4.cloned.1.call-update) | async-done | bytes 393232 | tf_op jit(solution)/shard_map/psum | solution.py:15
  249.0 111.2 %while.11 = (s32[]{:T(128)}, bf16[16,256,256]{2,1,0:T(8,128)(2,1)}, s32[]{:T(128)}, s32[16]{0:T(128)S(1)}, bf16[16,256,256]{2,1,0:T(8,128)(2,1)}, /*index=5*/s32...) while((s32[]{:T(128)}, bf16[16,256,256]{2,1,0:T(8,128)(2,1)}, ...), condition=%wide.region_18.19_spmd, body=%wide.region_16.18_spmd.sunk | while | flops 33816608 | bytes 656726 | solution.py:117
  249.7 0.7 dynamic_slice.36
  252.4 0.7 dynamic_slice.38
  255.2 0.7 dynamic_slice.37
  257.9 0.8 and_reduce_fusion.2
  258.7 2.6 fusion.49
  262.0 0.7 dynamic_slice.36
  264.7 0.7 dynamic_slice.38
  267.4 0.7 dynamic_slice.37
  270.2 0.8 and_reduce_fusion.2
  271.0 2.6 fusion.49
  274.2 0.7 dynamic_slice.36
  277.0 0.7 dynamic_slice.38
  279.7 0.7 dynamic_slice.37
  282.5 0.8 and_reduce_fusion.2
  283.3 2.6 fusion.49
  286.5 0.7 dynamic_slice.36
  292.0 0.7 dynamic_slice.37
  294.7 0.8 and_reduce_fusion.2
  295.5 2.6 fusion.49
  304.3 0.7 dynamic_slice.37
  307.0 0.8 and_reduce_fusion.2
  307.8 2.6 fusion.49
  316.6 0.7 dynamic_slice.37
  319.3 0.8 and_reduce_fusion.2
  320.1 2.6 fusion.49
  328.8 0.7 dynamic_slice.37
  331.6 0.8 and_reduce_fusion.2
  332.4 2.6 fusion.49
  341.1 0.7 dynamic_slice.37
  343.9 0.8 and_reduce_fusion.2
  344.7 2.6 fusion.49
  353.4 0.7 dynamic_slice.37
  356.2 0.8 and_reduce_fusion.2
  356.9 2.6 fusion.49
  (79 shorter events, 11.0 us)
Async XLA Ops:
  6.5 97.5 %all-reduce.6.cloned.1.call-start = ((), (), s32[]{:S(2)}) async-start(), calls=%async_computation.1 | async-start | bytes 4194304 | tf_op jit(solution)/shard_map/psum | solution.py:54
  7.2 3.0 copy-start.8
  7.2 3.0 copy-start
  10.1 2.4 copy-start.7
  17.9 231.1 %all-reduce.4.cloned.1.call-start = ((), (), s32[]{:S(2)}) async-start(), calls=%async_computation | async-start | bytes 786432 | tf_op jit(solution)/shard_map/psum | solution.py:15
  43.9 23.4 %copy-start.4 = (bf16[64,256]{1,0:T(8,128)(2,1)S(1)}, bf16[64,256]{1,0:T(8,128)(2,1)}, u32[]{:S(2)}) copy-start(bf16[64,256]{1,0:T(8,128)(2,1)} %param.15) | copy-start | bytes 98308
  43.9 29.3 %copy-start.5 = (bf16[256,32]{0,1:T(8,128)(2,1)S(1)}, bf16[256,32]{0,1:T(8,128)(2,1)}, u32[]{:S(2)}) copy-start(bf16[256,32]{0,1:T(8,128)(2,1)} %param.14) | copy-start | bytes 49156
  104.1 1.5 copy-start.3
  152.1 2.0 copy-start.1
  170.1 4.3 %copy-start.2 = (bf16[16,256,256]{2,0,1:T(8,128)(2,1)S(1)}, bf16[16,256,256]{2,0,1:T(8,128)(2,1)}, u32[]{:S(2)}) copy-start(bf16[16,256,256]{2,0,1:T(8,128)(2,1)} %get-tuple-element.145) | copy-start | bytes 6291460
  176.5 72.5 %copy-start.6 = (s32[3]{0:T(128)S(1)}, s32[3]{0:T(128)}, u32[]{:S(2)}) copy-start(s32[3]{0:T(128)} %constant.108.clone.1) | copy-start | bytes 40
Sparse Core Ops, SparseCore 0:
  18.0 54.8 all-reduce.5
  179.8 69.1 all-reduce.3
where the time goes:
time: 369 us; the launch traced here: 367 us
  local copies, waits for them, and re-layouts  109 us (30%)
  waiting for transfers between devices  64.8 us (18%)
  loops' own time  62.9 us (17%)
  blocking collectives  56.7 us (15%)
  matrix products  30.7 us (8%)
  other arithmetic  28.2 us (8%)
  between operations  14.4 us (4%)
    psum x1, waiting for transfers between devices, broadcast(): return lax.psum(kept, axis)  64.8 us
    another operation x1, loops' own time, body(): result = lax.fori_loop(0, needed, own_step, result)  62.9 us
    gather x2, local copies, waits for them, and re-layouts, pick_rows(): return tile[rows]  40.7 us
    all_gather x1, blocking collectives, body(): lower_inv = lax.all_gather(l_inverse, 'pcol', axis=1, tiled=True)  30.7 us
    dot_general x9, matrix products, trailing(): jnp.dot(lower_tile, upper_list[upper_index], preferred_element_type=jnp.f...  23.2 us
    gather x1, local copies, waits for them, and re-layouts, body(): anchor = anchor_top[row_index]  23 us
    select_n x1, other arithmetic, body(): jnp.where(upper_mask[:, None, None], upper_list[upper_pick], result)  16 us
    dynamic_slice x18, local copies, waits for them, and re-layouts, own_step(): value = trailing(primed[slot], got_list[lower_pick[slot]], upper_pick[slot])  12.1 us
  transfers between devices with their start and end apart: 2, of which 1 were waited for; matrix products, arithmetic and copies ran while one was open for 9% of the time, Pallas kernels for 0%

commit v1 on v0

--- a/solution.py
+++ b/solution.py
@@ -12,7 +12,7 @@
 
 def broadcast(value, axis, source):
     kept = jnp.where(lax.axis_index(axis) == source, value, 0).astype(value.dtype)
-    return lax.psum(kept, axis)
+    return jnp.sum(lax.all_gather(kept, axis), axis=0)
 
 
 def pick_rows(tile, rows):

time: 369 us -> 355 us (0.962)
  waiting for transfers between devices: 64.8 us -> 53.4 us
  loops' own time: 62.9 us -> 58.6 us
    psum x1 -> x0, waiting for transfers between devices: 64.8 us -> none  [broadcast(): return lax.psum(kept, axis)]
    all_gather x0 -> x1, waiting for transfers between devices: none -> 53.4 us  [broadcast(): return jnp.sum(lax.all_gather(kept, axis), axis=0)]
    psum x1 -> x0, blocking collectives: 11.6 us -> none  [broadcast(): return lax.psum(kept, axis)]
    unnamed x0 -> x1, blocking collectives: none -> 11.6 us
    another operation x1, loops' own time: 62.9 us -> 58.6 us  [body(): result = lax.fori_loop(0, needed, own_step, result)]
  transfers between devices with their start and end apart: 2 -> 2, of which waited for: 1 -> 1; matrix products, arithmetic and copies ran while one was open for 9% -> 10% of each run, Pallas kernels for 0% -> 0%
where the time goes in v1:
time: 355 us; the launch traced here: 353 us
  local copies, waits for them, and re-layouts  110 us (31%)
  loops' own time  58.6 us (17%)
  blocking collectives  56.1 us (16%)
  waiting for transfers between devices  53.4 us (15%)
  other arithmetic  30.7 us (9%)
  matrix products  29.6 us (8%)
  between operations  15.1 us (4%)
    another operation x1, loops' own time, body(): result = lax.fori_loop(0, needed, own_step, result)  58.6 us
    all_gather x1, waiting for transfers between devices, broadcast(): return jnp.sum(lax.all_gather(kept, axis), axis=0)  53.4 us
    gather x2, local copies, waits for them, and re-layouts, pick_rows(): return tile[rows]  40.7 us
    all_gather x1, blocking collectives, body(): lower_inv = lax.all_gather(l_inverse, 'pcol', axis=1, tiled=True)  30.7 us
    gather x1, local copies, waits for them, and re-layouts, body(): anchor = anchor_top[row_index]  23 us
    dot_general x9, matrix products, trailing(): jnp.dot(lower_tile, upper_list[upper_index], preferred_element_type=jnp.f...  22.1 us
    select_n x1, other arithmetic, body(): jnp.where(upper_mask[:, None, None], upper_list[upper_pick], result)  16 us
    dynamic_slice x18, local copies, waits for them, and re-layouts, own_step(): value = trailing(primed[slot], got_list[lower_pick[slot]], upper_pick[slot])  11.8 us
  transfers between devices with their start and end apart: 2, of which 1 were waited for; matrix products, arithmetic and copies ran while one was open for 10% of the time, Pallas kernels for 0%

profile of v1, /device:TPU:0, one launch (start us, length us, event | category | flops | bytes accessed | tf_op | source)
XLA Modules:
  0.0 353.1 jit_solution(16598737117220489840)
XLA Ops:
  7.2 2.9 copy.101
  10.2 2.2 convolution_convert_fusion
  12.8 2.1 gather_fusion.1
  14.9 3.0 fusion.11
  17.9 8.4 %psum.21 = bf16[8]{0:T(256)(128)(2,1)S(1)} all-reduce(bf16[8]{0:T(256)(128)(2,1)S(1)} %multiply_reduce_fusion), channel_id=1, replica_groups=mesh['prow'=4,'pcol'=8] {'prow'}, use_global_device_ids=true, to_apply=%region_1.2 | all-reduce | flops 8 | bytes 32 | tf_op jit(solution)/shard_map/psum | solution.py:56
  26.4 1.0 sort.48
  28.0 1.2 sort.49
  32.0 11.6 %all-reduce = s32[24]{0:T(128)S(1)} all-reduce(s32[24]{0:T(128)S(1)} %fusion.35), channel_id=2, replica_groups=mesh['prow'=4,'pcol'=8] {'pcol'}, use_global_device_ids=true, to_apply=%add | all-reduce | flops 24 | bytes 192
  43.9 1.4 scatter_custom_fusion
  45.4 23.0 %gather_fusion.5 = s32[4096]{0:T(1024)S(1)} fusion(s32[16384]{0:T(1024)S(1)} %scatter_custom_fusion, s32[4096]{0:T(1024)S(1)} %broadcast_clamp_fusion), kind=kCustom, calls=%fused_computation.5 | custom fusion | bytes 49152 | tf_op jit(solution)/shard_map/gather | solution.py:66
  68.7 5.4 %all_gather.17 = bf16[256,256]{1,0:T(8,128)(2,1)S(1)} all-gather(bf16[64,256]{1,0:T(8,128)(2,1)S(1)} %copy-done.4), channel_id=1, replica_groups=mesh['prow'=4,'pcol'=8] {'prow'}, dimensions={0}, use_global_device_ids=true | all-gather | bytes 163840 | tf_op jit(solution)/shard_map/all_gather | solution.py:38
  74.2 30.7 %all_gather.16 = bf16[256,256]{0,1:T(8,128)(2,1)S(1)} all-gather(bf16[256,32]{0,1:T(8,128)(2,1)S(1)} %copy-done.5), channel_id=1, replica_groups=mesh['prow'=4,'pcol'=8] {'pcol'}, dimensions={1}, use_global_device_ids=true | all-gather | bytes 147456 | tf_op jit(solution)/shard_map/all_gather | solution.py:39
  105.0 1.5 copy.77
  106.8 1.3 gather_fusion.2
  108.1 2.0 gather_fusion.4
  110.1 0.7 gather_fusion.6
  110.8 1.3 fusion.14
  112.3 40.7 %gather_fusion.11 = bf16[4096,256]{1,0:T(8,128)(2,1)} fusion(bf16[16,256,256]{2,1,0:T(8,128)(2,1)S(1)} %gather_fusion.6, s32[4096]{0:T(1024)S(1)} %bitcast.107), kind=kCustom, calls=%fused_computation.11 | custom fusion | bytes 4227072 | tf_op jit(solution)/shard_map/vmap()/gather | solution.py:19
  153.0 2.0 gather_fusion.3
  155.0 16.0 %copy_select_fusion = (bf16[16,256,256]{2,0,1:T(8,128)(2,1)}, bf16[16,256,256]{2,0,1:T(8,128)(2,1)S(1)}) fusion(bf16[16,256,256]{2,1,0:T(8,128)(2,1)} %gather_fusion.3, pred[16]{0:T(512)(128)(4,1)S(1)} %iota_compare_fusion.1, pred[16]{0:T(512)(128)(4,1)S(1)} %get-tuple-element.164, bf16[1,1,16,256,256]{4,3,2,1,0:T(8,128)(2,1)S(1)} %copy-done.1, ...), kind=kLoop, calls=%fused_computation.27 | loop fusion | flops 4194304 | bytes 12587056 | tf_op jit(solution)/shard_map/jit(_where)/select_n | solution.py:100
  171.0 2.1 copy.81
  173.2 2.2 gather_fusion.8
  175.3 2.1 copy.83
  177.4 2.2 gather_fusion.9
  179.6 1.0 broadcast_select_fusion.1
  180.6 1.3 sort.50
  182.0 0.7 convert_reduce_fusion
  182.7 2.4 scatter_fusion
  185.2 53.4 %all-gather.4.cloned.1.call-done = bf16[24,256,256]{2,1,0:T(8,128)(2,1)} async-done(((bf16[3,256,256]{2,1,0:T(8,128)(2,1)}), bf16[24,256,256]{2,1,0:T(8,128)(2,1)}) %all-gather.4.cloned.1.call-update) | async-done | bytes 3145744 | tf_op jit(solution)/shard_map/all_gather | solution.py:15
  238.5 2.4 reduce_sum.65
  240.9 105.3 %while.11 = (s32[]{:T(128)}, bf16[16,256,256]{2,1,0:T(8,128)(2,1)}, s32[]{:T(128)}, s32[16]{0:T(128)S(1)}, bf16[16,256,256]{2,1,0:T(8,128)(2,1)}, /*index=5*/s32...) while((s32[]{:T(128)}, bf16[16,256,256]{2,1,0:T(8,128)(2,1)}, ...), condition=%wide.region_18.19_spmd, body=%wide.region_16.18_spmd.sunk | while | flops 33816608 | bytes 656726 | solution.py:117
  246.8 0.7 dynamic_slice.37
  249.3 0.8 and_reduce_fusion.2
  250.1 2.5 fusion.50
  258.4 0.7 dynamic_slice.37
  261.0 0.8 and_reduce_fusion.2
  261.7 2.5 fusion.50
  264.9 0.7 dynamic_slice.36
  267.5 0.7 dynamic_slice.38
  270.0 0.7 dynamic_slice.37
  272.6 0.8 and_reduce_fusion.2
  273.4 2.5 fusion.50
  281.6 0.7 dynamic_slice.37
  284.2 0.8 and_reduce_fusion.2
  285.0 2.5 fusion.50
  293.3 0.7 dynamic_slice.37
  295.8 0.8 and_reduce_fusion.2
  296.6 2.5 fusion.50
  299.8 0.7 dynamic_slice.36
  302.3 0.7 dynamic_slice.38
  304.9 0.7 dynamic_slice.37
  307.5 0.8 and_reduce_fusion.2
  308.2 2.5 fusion.50
  316.5 0.7 dynamic_slice.37
  319.1 0.8 and_reduce_fusion.2
  319.9 2.5 fusion.50
  328.2 0.7 dynamic_slice.37
  330.7 0.8 and_reduce_fusion.2
  331.5 2.5 fusion.50
  334.7 0.7 dynamic_slice.36
  337.2 0.7 dynamic_slice.38
  339.8 0.7 dynamic_slice.37
  342.3 0.8 and_reduce_fusion.2
  343.1 2.5 fusion.50
  (86 shorter events, 12.3 us)
Async XLA Ops:
  6.5 98.5 %all-reduce.4.cloned.1.call-start = ((), (), s32[]{:S(2)}) async-start(), calls=%async_computation.1 | async-start | bytes 4194304 | tf_op jit(solution)/shard_map/psum | solution.py:54
  7.2 3.0 copy-start.8
  7.2 3.0 copy-start
  10.1 2.4 copy-start.7
  17.9 12.7 %copy-start.9 = (u32[32]{0:T(128)S(1)}, u32[32]{0:T(128)}, u32[]{:S(2)}) copy-start(u32[32]{0:T(128)} %constant.147) | copy-start | bytes 388
  17.9 220.6 %all-gather.4.cloned.1.call-start = ((), (), s32[]{:S(2)}) async-start(), calls=%async_computation | async-start | bytes 3538944 | tf_op jit(solution)/shard_map/all_gather | solution.py:15
  45.4 23.4 %copy-start.4 = (bf16[64,256]{1,0:T(8,128)(2,1)S(1)}, bf16[64,256]{1,0:T(8,128)(2,1)}, u32[]{:S(2)}) copy-start(bf16[64,256]{1,0:T(8,128)(2,1)} %param.15) | copy-start | bytes 98308
  45.4 28.8 %copy-start.5 = (bf16[256,32]{0,1:T(8,128)(2,1)S(1)}, bf16[256,32]{0,1:T(8,128)(2,1)}, u32[]{:S(2)}) copy-start(bf16[256,32]{0,1:T(8,128)(2,1)} %param.14) | copy-start | bytes 49156
  105.0 1.5 copy-start.3
  153.0 2.0 copy-start.1
  171.0 4.3 %copy-start.2 = (bf16[16,256,256]{2,0,1:T(8,128)(2,1)S(1)}, bf16[16,256,256]{2,0,1:T(8,128)(2,1)}, u32[]{:S(2)}) copy-start(bf16[16,256,256]{2,0,1:T(8,128)(2,1)} %get-tuple-element.154) | copy-start | bytes 6291460
  182.7 58.2 %copy-start.6 = (s32[3]{0:T(128)S(1)}, s32[3]{0:T(128)}, u32[]{:S(2)}) copy-start(s32[3]{0:T(128)} %constant.109.clone.1) | copy-start | bytes 40
Sparse Core Ops, SparseCore 0:
  18.0 54.5 all-reduce.3
  180.7 57.7 all-gather.3
